TPU v7x, 8 devices: a whole 2x2x1 slice. The times are simulated.
8 devices in a mesh: rep: 1 (over z), sub: 2 (over y), blk: 4 (over x, core).
Axes of the slice: x: 2, y: 2, z: 1, core: 2. Of those that a mesh axis runs over, the one named last changes fastest.
Arguments:
- ratings: float32 [8192, 4096], P(('rep', 'blk', 'sub'))
- mask: int32 [8192, 4096], P(('rep', 'blk', 'sub'))
- user_init: float32 [8192, 96], P(('rep', 'blk', 'sub'))
- item_init: float32 [4096, 96], P(('rep', 'blk'))
Outputs:
- output 1: float32 [8192, 96], P(('rep', 'blk', 'sub'))
- output 2: float32 [4096, 96], P(('rep', 'blk'))
All inputs are finite; a program needn't handle non-finite values.
Results may differ from a plain program's by a relative error of at most 0.001.
Values are sent between devices in bfloat16 or wider.
A program may use at most 1 GiB of HBM per device.

v0:
```python
import math
import jax
import jax.numpy as jnp
from jax import lax
from jax.sharding import PartitionSpec as P

STEPS = 4
EPOCHS = 2
STEP_GAIN = 0.4
DECAY = 0.002


def solution(mesh):
    blk_size = mesh.shape['blk']
    sub_size = mesh.shape['sub']
    row_spec = P(('rep', 'blk', 'sub'), None)
    item_spec = P(('rep', 'blk'), None)
    prev_pairs = [(source_idx, (source_idx - 1) % blk_size) for source_idx in range(blk_size)]

    def local_run(ratings, mask, user_init, item_init):
        users_dev = ratings.shape[0]
        items_dev, factor_dim = item_init.shape
        big_side = max(items_dev, sub_size * users_dev)
        step_size = STEP_GAIN * math.sqrt(factor_dim) / (math.sqrt(big_side) + math.sqrt(factor_dim)) ** 2
        decay_coef = DECAY / step_size
        blk_pos = lax.axis_index('blk')

        def sub_epoch(counter, state):
            user_st, item_st = state
            col_start = ((blk_pos + counter) % blk_size) * items_dev
            rating_now = lax.dynamic_slice_in_dim(ratings, col_start, items_dev, axis=1)
            mask_now = lax.dynamic_slice_in_dim(mask, col_start, items_dev, axis=1) != 0
            for step_idx in range(STEPS):
                user_half = user_st.astype(jnp.bfloat16)
                item_half = item_st.astype(jnp.bfloat16)
                predicted = lax.dot_general(user_half, item_half, (((1,), (1,)), ((), ())), preferred_element_type=jnp.float32)
                err_half = jnp.where(mask_now, predicted - rating_now, 0.0).astype(jnp.bfloat16)
                grad_user = jnp.dot(err_half, item_half, preferred_element_type=jnp.float32) + decay_coef * user_st
                part_item = lax.dot_general(err_half, user_half, (((0,), (0,)), ((), ())), preferred_element_type=jnp.float32)
                grad_item = lax.psum(part_item, 'sub') + decay_coef * item_st
                user_st = user_st - step_size * grad_user
                item_st = item_st - step_size * grad_item
            return user_st, lax.ppermute(item_st, 'blk', prev_pairs)

        return lax.fori_loop(0, EPOCHS * blk_size, sub_epoch, (user_init, item_init))

    return jax.shard_map(local_run, mesh=mesh, in_specs=(row_spec, row_spec, row_spec, item_spec), out_specs=(row_spec, item_spec), check_vma=False)
```

profile of v0, /device:TPU:0, one launch (start us, length us, event | category | flops | bytes accessed | tf_op | source)
XLA Modules:
  0.0 936.4 jit_solution(12014723385407120006)
XLA Ops:
  10.7 917.4 %while.17 = (s32[]{:T(128)}, f32[1024,96]{0,1:T(8,128)}, f32[1024,96]{0,1:T(8,128)}, s32[]{:T(128)}, s32[1024,4096]{1,0:T(8,128)}, /*index=5*/f32[1024,4096]{1,0...) while((s32[]{:T(128)}, f32[1024,96]{0,1:T(8,128)}, ...), condition=%wide.region_5.6_spmd, body=%wide.region_0.5_spmd.sunk | while | flops 2435252224 | bytes 86377144 | solution.py:45
  13.4 3.3 select_convert_fusion.8
  20.9 21.0 %all-reduce.5.cloned.1.call-done = f32[1024,96]{0,1:T(8,128)} async-done(((f32[1024,96]{0,1:T(8,128)}), f32[1024,96]{0,1:T(8,128)}) %all-reduce.5.cloned.1.call-update) | async-done | bytes 393232 | tf_op jit(solution)/shard_map/while/body/eval_jaxpr/psum | solution.py:40
  50.0 17.7 %all-reduce.7.cloned.1.call-done = f32[1024,96]{0,1:T(8,128)} async-done(((f32[1024,96]{0,1:T(8,128)}), f32[1024,96]{0,1:T(8,128)}) %all-reduce.7.cloned.1.call-update) | async-done | bytes 393232 | tf_op jit(solution)/shard_map/while/body/eval_jaxpr/psum | solution.py:40
  76.1 17.6 %all-reduce.9.cloned.1.call-done = f32[1024,96]{0,1:T(8,128)} async-done(((f32[1024,96]{0,1:T(8,128)}), f32[1024,96]{0,1:T(8,128)}) %all-reduce.9.cloned.1.call-update) | async-done | bytes 393232 | tf_op jit(solution)/shard_map/while/body/eval_jaxpr/psum | solution.py:40
  99.2 20.1 %all-reduce.11.cloned.1.call-done = f32[1024,96]{0,1:T(8,128)} async-done(((f32[1024,96]{0,1:T(8,128)}), f32[1024,96]{0,1:T(8,128)}) %all-reduce.11.cloned.1.call-update) | async-done | bytes 393232 | tf_op jit(solution)/shard_map/while/body/eval_jaxpr/psum | solution.py:40
  123.7 3.7 collective-permute-done
  130.2 3.3 select_convert_fusion.8
  137.6 18.7 %all-reduce.5.cloned.1.call-done = f32[1024,96]{0,1:T(8,128)} async-done(((f32[1024,96]{0,1:T(8,128)}), f32[1024,96]{0,1:T(8,128)}) %all-reduce.5.cloned.1.call-update) | async-done | bytes 393232 | tf_op jit(solution)/shard_map/while/body/eval_jaxpr/psum | solution.py:40
  164.4 17.7 %all-reduce.7.cloned.1.call-done = f32[1024,96]{0,1:T(8,128)} async-done(((f32[1024,96]{0,1:T(8,128)}), f32[1024,96]{0,1:T(8,128)}) %all-reduce.7.cloned.1.call-update) | async-done | bytes 393232 | tf_op jit(solution)/shard_map/while/body/eval_jaxpr/psum | solution.py:40
  190.5 17.6 %all-reduce.9.cloned.1.call-done = f32[1024,96]{0,1:T(8,128)} async-done(((f32[1024,96]{0,1:T(8,128)}), f32[1024,96]{0,1:T(8,128)}) %all-reduce.9.cloned.1.call-update) | async-done | bytes 393232 | tf_op jit(solution)/shard_map/while/body/eval_jaxpr/psum | solution.py:40
  213.6 20.1 %all-reduce.11.cloned.1.call-done = f32[1024,96]{0,1:T(8,128)} async-done(((f32[1024,96]{0,1:T(8,128)}), f32[1024,96]{0,1:T(8,128)}) %all-reduce.11.cloned.1.call-update) | async-done | bytes 393232 | tf_op jit(solution)/shard_map/while/body/eval_jaxpr/psum | solution.py:40
  238.1 3.7 collective-permute-done
  244.5 3.3 select_convert_fusion.8
  252.0 18.7 %all-reduce.5.cloned.1.call-done = f32[1024,96]{0,1:T(8,128)} async-done(((f32[1024,96]{0,1:T(8,128)}), f32[1024,96]{0,1:T(8,128)}) %all-reduce.5.cloned.1.call-update) | async-done | bytes 393232 | tf_op jit(solution)/shard_map/while/body/eval_jaxpr/psum | solution.py:40
  278.8 17.7 %all-reduce.7.cloned.1.call-done = f32[1024,96]{0,1:T(8,128)} async-done(((f32[1024,96]{0,1:T(8,128)}), f32[1024,96]{0,1:T(8,128)}) %all-reduce.7.cloned.1.call-update) | async-done | bytes 393232 | tf_op jit(solution)/shard_map/while/body/eval_jaxpr/psum | solution.py:40
  304.8 17.6 %all-reduce.9.cloned.1.call-done = f32[1024,96]{0,1:T(8,128)} async-done(((f32[1024,96]{0,1:T(8,128)}), f32[1024,96]{0,1:T(8,128)}) %all-reduce.9.cloned.1.call-update) | async-done | bytes 393232 | tf_op jit(solution)/shard_map/while/body/eval_jaxpr/psum | solution.py:40
  328.0 20.1 %all-reduce.11.cloned.1.call-done = f32[1024,96]{0,1:T(8,128)} async-done(((f32[1024,96]{0,1:T(8,128)}), f32[1024,96]{0,1:T(8,128)}) %all-reduce.11.cloned.1.call-update) | async-done | bytes 393232 | tf_op jit(solution)/shard_map/while/body/eval_jaxpr/psum | solution.py:40
  352.4 3.7 collective-permute-done
  358.9 3.3 select_convert_fusion.8
  366.4 18.7 %all-reduce.5.cloned.1.call-done = f32[1024,96]{0,1:T(8,128)} async-done(((f32[1024,96]{0,1:T(8,128)}), f32[1024,96]{0,1:T(8,128)}) %all-reduce.5.cloned.1.call-update) | async-done | bytes 393232 | tf_op jit(solution)/shard_map/while/body/eval_jaxpr/psum | solution.py:40
  393.1 17.7 %all-reduce.7.cloned.1.call-done = f32[1024,96]{0,1:T(8,128)} async-done(((f32[1024,96]{0,1:T(8,128)}), f32[1024,96]{0,1:T(8,128)}) %all-reduce.7.cloned.1.call-update) | async-done | bytes 393232 | tf_op jit(solution)/shard_map/while/body/eval_jaxpr/psum | solution.py:40
  419.2 17.6 %all-reduce.9.cloned.1.call-done = f32[1024,96]{0,1:T(8,128)} async-done(((f32[1024,96]{0,1:T(8,128)}), f32[1024,96]{0,1:T(8,128)}) %all-reduce.9.cloned.1.call-update) | async-done | bytes 393232 | tf_op jit(solution)/shard_map/while/body/eval_jaxpr/psum | solution.py:40
  442.4 20.1 %all-reduce.11.cloned.1.call-done = f32[1024,96]{0,1:T(8,128)} async-done(((f32[1024,96]{0,1:T(8,128)}), f32[1024,96]{0,1:T(8,128)}) %all-reduce.11.cloned.1.call-update) | async-done | bytes 393232 | tf_op jit(solution)/shard_map/while/body/eval_jaxpr/psum | solution.py:40
  466.8 3.7 collective-permute-done
  473.3 3.3 select_convert_fusion.8
  480.8 18.7 %all-reduce.5.cloned.1.call-done = f32[1024,96]{0,1:T(8,128)} async-done(((f32[1024,96]{0,1:T(8,128)}), f32[1024,96]{0,1:T(8,128)}) %all-reduce.5.cloned.1.call-update) | async-done | bytes 393232 | tf_op jit(solution)/shard_map/while/body/eval_jaxpr/psum | solution.py:40
  507.5 17.7 %all-reduce.7.cloned.1.call-done = f32[1024,96]{0,1:T(8,128)} async-done(((f32[1024,96]{0,1:T(8,128)}), f32[1024,96]{0,1:T(8,128)}) %all-reduce.7.cloned.1.call-update) | async-done | bytes 393232 | tf_op jit(solution)/shard_map/while/body/eval_jaxpr/psum | solution.py:40
  533.6 17.6 %all-reduce.9.cloned.1.call-done = f32[1024,96]{0,1:T(8,128)} async-done(((f32[1024,96]{0,1:T(8,128)}), f32[1024,96]{0,1:T(8,128)}) %all-reduce.9.cloned.1.call-update) | async-done | bytes 393232 | tf_op jit(solution)/shard_map/while/body/eval_jaxpr/psum | solution.py:40
  556.8 20.1 %all-reduce.11.cloned.1.call-done = f32[1024,96]{0,1:T(8,128)} async-done(((f32[1024,96]{0,1:T(8,128)}), f32[1024,96]{0,1:T(8,128)}) %all-reduce.11.cloned.1.call-update) | async-done | bytes 393232 | tf_op jit(solution)/shard_map/while/body/eval_jaxpr/psum | solution.py:40
  581.2 3.7 collective-permute-done
  587.7 3.3 select_convert_fusion.8
  595.2 18.7 %all-reduce.5.cloned.1.call-done = f32[1024,96]{0,1:T(8,128)} async-done(((f32[1024,96]{0,1:T(8,128)}), f32[1024,96]{0,1:T(8,128)}) %all-reduce.5.cloned.1.call-update) | async-done | bytes 393232 | tf_op jit(solution)/shard_map/while/body/eval_jaxpr/psum | solution.py:40
  621.9 17.7 %all-reduce.7.cloned.1.call-done = f32[1024,96]{0,1:T(8,128)} async-done(((f32[1024,96]{0,1:T(8,128)}), f32[1024,96]{0,1:T(8,128)}) %all-reduce.7.cloned.1.call-update) | async-done | bytes 393232 | tf_op jit(solution)/shard_map/while/body/eval_jaxpr/psum | solution.py:40
  648.0 17.6 %all-reduce.9.cloned.1.call-done = f32[1024,96]{0,1:T(8,128)} async-done(((f32[1024,96]{0,1:T(8,128)}), f32[1024,96]{0,1:T(8,128)}) %all-reduce.9.cloned.1.call-update) | async-done | bytes 393232 | tf_op jit(solution)/shard_map/while/body/eval_jaxpr/psum | solution.py:40
  671.2 20.1 %all-reduce.11.cloned.1.call-done = f32[1024,96]{0,1:T(8,128)} async-done(((f32[1024,96]{0,1:T(8,128)}), f32[1024,96]{0,1:T(8,128)}) %all-reduce.11.cloned.1.call-update) | async-done | bytes 393232 | tf_op jit(solution)/shard_map/while/body/eval_jaxpr/psum | solution.py:40
  695.6 3.7 collective-permute-done
  702.1 3.3 select_convert_fusion.8
  709.6 18.7 %all-reduce.5.cloned.1.call-done = f32[1024,96]{0,1:T(8,128)} async-done(((f32[1024,96]{0,1:T(8,128)}), f32[1024,96]{0,1:T(8,128)}) %all-reduce.5.cloned.1.call-update) | async-done | bytes 393232 | tf_op jit(solution)/shard_map/while/body/eval_jaxpr/psum | solution.py:40
  736.3 17.7 %all-reduce.7.cloned.1.call-done = f32[1024,96]{0,1:T(8,128)} async-done(((f32[1024,96]{0,1:T(8,128)}), f32[1024,96]{0,1:T(8,128)}) %all-reduce.7.cloned.1.call-update) | async-done | bytes 393232 | tf_op jit(solution)/shard_map/while/body/eval_jaxpr/psum | solution.py:40
  762.4 17.6 %all-reduce.9.cloned.1.call-done = f32[1024,96]{0,1:T(8,128)} async-done(((f32[1024,96]{0,1:T(8,128)}), f32[1024,96]{0,1:T(8,128)}) %all-reduce.9.cloned.1.call-update) | async-done | bytes 393232 | tf_op jit(solution)/shard_map/while/body/eval_jaxpr/psum | solution.py:40
  785.6 20.1 %all-reduce.11.cloned.1.call-done = f32[1024,96]{0,1:T(8,128)} async-done(((f32[1024,96]{0,1:T(8,128)}), f32[1024,96]{0,1:T(8,128)}) %all-reduce.11.cloned.1.call-update) | async-done | bytes 393232 | tf_op jit(solution)/shard_map/while/body/eval_jaxpr/psum | solution.py:40
  810.0 3.7 collective-permute-done
  823.9 18.7 %all-reduce.5.cloned.1.call-done = f32[1024,96]{0,1:T(8,128)} async-done(((f32[1024,96]{0,1:T(8,128)}), f32[1024,96]{0,1:T(8,128)}) %all-reduce.5.cloned.1.call-update) | async-done | bytes 393232 | tf_op jit(solution)/shard_map/while/body/eval_jaxpr/psum | solution.py:40
  850.7 17.7 %all-reduce.7.cloned.1.call-done = f32[1024,96]{0,1:T(8,128)} async-done(((f32[1024,96]{0,1:T(8,128)}), f32[1024,96]{0,1:T(8,128)}) %all-reduce.7.cloned.1.call-update) | async-done | bytes 393232 | tf_op jit(solution)/shard_map/while/body/eval_jaxpr/psum | solution.py:40
  876.8 17.6 %all-reduce.9.cloned.1.call-done = f32[1024,96]{0,1:T(8,128)} async-done(((f32[1024,96]{0,1:T(8,128)}), f32[1024,96]{0,1:T(8,128)}) %all-reduce.9.cloned.1.call-update) | async-done | bytes 393232 | tf_op jit(solution)/shard_map/while/body/eval_jaxpr/psum | solution.py:40
  899.9 20.1 %all-reduce.11.cloned.1.call-done = f32[1024,96]{0,1:T(8,128)} async-done(((f32[1024,96]{0,1:T(8,128)}), f32[1024,96]{0,1:T(8,128)}) %all-reduce.11.cloned.1.call-update) | async-done | bytes 393232 | tf_op jit(solution)/shard_map/while/body/eval_jaxpr/psum | solution.py:40
  924.4 3.7 collective-permute-done
  (316 shorter events, 273.5 us)
Async XLA Ops:
  10.7 31.2 %all-reduce.5.cloned.1.call-start = ((), (), s32[]{:S(2)}) async-start(), calls=%async_computation | async-start | bytes 786432 | tf_op jit(solution)/shard_map/while/body/eval_jaxpr/psum | solution.py:40
  19.0 48.7 %all-reduce.7.cloned.1.call-start = ((), (), s32[]{:S(2)}) async-start(), calls=%async_computation.1 | async-start | bytes 786432 | tf_op jit(solution)/shard_map/while/body/eval_jaxpr/psum | solution.py:40
  47.5 46.2 %all-reduce.9.cloned.1.call-start = ((), (), s32[]{:S(2)}) async-start(), calls=%async_computation.2 | async-start | bytes 786432 | tf_op jit(solution)/shard_map/while/body/eval_jaxpr/psum | solution.py:40
  73.5 45.9 %all-reduce.11.cloned.1.call-start = ((), (), s32[]{:S(2)}) async-start(), calls=%async_computation.3 | async-start | bytes 786432 | tf_op jit(solution)/shard_map/while/body/eval_jaxpr/psum | solution.py:40
  98.0 24.2 %copy-start.1 = (f32[1024,96]{0,1:T(8,128)S(1)}, f32[1024,96]{0,1:T(8,128)}, u32[]{:S(2)}) copy-start(f32[1024,96]{0,1:T(8,128)} %fusion.101) | copy-start | bytes 1179652 | tf_op jit(solution)/shard_map/while
  121.2 6.2 collective-permute-start
  127.4 28.9 %all-reduce.5.cloned.1.call-start = ((), (), s32[]{:S(2)}) async-start(), calls=%async_computation | async-start | bytes 786432 | tf_op jit(solution)/shard_map/while/body/eval_jaxpr/psum | solution.py:40
  135.7 46.4 %all-reduce.7.cloned.1.call-start = ((), (), s32[]{:S(2)}) async-start(), calls=%async_computation.1 | async-start | bytes 786432 | tf_op jit(solution)/shard_map/while/body/eval_jaxpr/psum | solution.py:40
  161.9 46.2 %all-reduce.9.cloned.1.call-start = ((), (), s32[]{:S(2)}) async-start(), calls=%async_computation.2 | async-start | bytes 786432 | tf_op jit(solution)/shard_map/while/body/eval_jaxpr/psum | solution.py:40
  187.9 45.9 %all-reduce.11.cloned.1.call-start = ((), (), s32[]{:S(2)}) async-start(), calls=%async_computation.3 | async-start | bytes 786432 | tf_op jit(solution)/shard_map/while/body/eval_jaxpr/psum | solution.py:40
  212.4 24.2 %copy-start.1 = (f32[1024,96]{0,1:T(8,128)S(1)}, f32[1024,96]{0,1:T(8,128)}, u32[]{:S(2)}) copy-start(f32[1024,96]{0,1:T(8,128)} %fusion.101) | copy-start | bytes 1179652 | tf_op jit(solution)/shard_map/while
  235.6 6.2 collective-permute-start
  241.8 28.9 %all-reduce.5.cloned.1.call-start = ((), (), s32[]{:S(2)}) async-start(), calls=%async_computation | async-start | bytes 786432 | tf_op jit(solution)/shard_map/while/body/eval_jaxpr/psum | solution.py:40
  250.1 46.4 %all-reduce.7.cloned.1.call-start = ((), (), s32[]{:S(2)}) async-start(), calls=%async_computation.1 | async-start | bytes 786432 | tf_op jit(solution)/shard_map/while/body/eval_jaxpr/psum | solution.py:40
  276.2 46.2 %all-reduce.9.cloned.1.call-start = ((), (), s32[]{:S(2)}) async-start(), calls=%async_computation.2 | async-start | bytes 786432 | tf_op jit(solution)/shard_map/while/body/eval_jaxpr/psum | solution.py:40
  302.3 45.9 %all-reduce.11.cloned.1.call-start = ((), (), s32[]{:S(2)}) async-start(), calls=%async_computation.3 | async-start | bytes 786432 | tf_op jit(solution)/shard_map/while/body/eval_jaxpr/psum | solution.py:40
  326.7 24.2 %copy-start.1 = (f32[1024,96]{0,1:T(8,128)S(1)}, f32[1024,96]{0,1:T(8,128)}, u32[]{:S(2)}) copy-start(f32[1024,96]{0,1:T(8,128)} %fusion.101) | copy-start | bytes 1179652 | tf_op jit(solution)/shard_map/while
  350.0 6.2 collective-permute-start
  356.2 28.9 %all-reduce.5.cloned.1.call-start = ((), (), s32[]{:S(2)}) async-start(), calls=%async_computation | async-start | bytes 786432 | tf_op jit(solution)/shard_map/while/body/eval_jaxpr/psum | solution.py:40
  364.4 46.4 %all-reduce.7.cloned.1.call-start = ((), (), s32[]{:S(2)}) async-start(), calls=%async_computation.1 | async-start | bytes 786432 | tf_op jit(solution)/shard_map/while/body/eval_jaxpr/psum | solution.py:40
  390.6 46.2 %all-reduce.9.cloned.1.call-start = ((), (), s32[]{:S(2)}) async-start(), calls=%async_computation.2 | async-start | bytes 786432 | tf_op jit(solution)/shard_map/while/body/eval_jaxpr/psum | solution.py:40
  416.7 45.9 %all-reduce.11.cloned.1.call-start = ((), (), s32[]{:S(2)}) async-start(), calls=%async_computation.3 | async-start | bytes 786432 | tf_op jit(solution)/shard_map/while/body/eval_jaxpr/psum | solution.py:40
  441.1 24.2 %copy-start.1 = (f32[1024,96]{0,1:T(8,128)S(1)}, f32[1024,96]{0,1:T(8,128)}, u32[]{:S(2)}) copy-start(f32[1024,96]{0,1:T(8,128)} %fusion.101) | copy-start | bytes 1179652 | tf_op jit(solution)/shard_map/while
  464.4 6.2 collective-permute-start
  470.6 28.9 %all-reduce.5.cloned.1.call-start = ((), (), s32[]{:S(2)}) async-start(), calls=%async_computation | async-start | bytes 786432 | tf_op jit(solution)/shard_map/while/body/eval_jaxpr/psum | solution.py:40
  478.8 46.4 %all-reduce.7.cloned.1.call-start = ((), (), s32[]{:S(2)}) async-start(), calls=%async_computation.1 | async-start | bytes 786432 | tf_op jit(solution)/shard_map/while/body/eval_jaxpr/psum | solution.py:40
  505.0 46.2 %all-reduce.9.cloned.1.call-start = ((), (), s32[]{:S(2)}) async-start(), calls=%async_computation.2 | async-start | bytes 786432 | tf_op jit(solution)/shard_map/while/body/eval_jaxpr/psum | solution.py:40
  531.0 45.9 %all-reduce.11.cloned.1.call-start = ((), (), s32[]{:S(2)}) async-start(), calls=%async_computation.3 | async-start | bytes 786432 | tf_op jit(solution)/shard_map/while/body/eval_jaxpr/psum | solution.py:40
  555.5 24.2 %copy-start.1 = (f32[1024,96]{0,1:T(8,128)S(1)}, f32[1024,96]{0,1:T(8,128)}, u32[]{:S(2)}) copy-start(f32[1024,96]{0,1:T(8,128)} %fusion.101) | copy-start | bytes 1179652 | tf_op jit(solution)/shard_map/while
  578.8 6.2 collective-permute-start
  585.0 28.9 %all-reduce.5.cloned.1.call-start = ((), (), s32[]{:S(2)}) async-start(), calls=%async_computation | async-start | bytes 786432 | tf_op jit(solution)/shard_map/while/body/eval_jaxpr/psum | solution.py:40
  593.2 46.4 %all-reduce.7.cloned.1.call-start = ((), (), s32[]{:S(2)}) async-start(), calls=%async_computation.1 | async-start | bytes 786432 | tf_op jit(solution)/shard_map/while/body/eval_jaxpr/psum | solution.py:40
  619.4 46.2 %all-reduce.9.cloned.1.call-start = ((), (), s32[]{:S(2)}) async-start(), calls=%async_computation.2 | async-start | bytes 786432 | tf_op jit(solution)/shard_map/while/body/eval_jaxpr/psum | solution.py:40
  645.4 45.9 %all-reduce.11.cloned.1.call-start = ((), (), s32[]{:S(2)}) async-start(), calls=%async_computation.3 | async-start | bytes 786432 | tf_op jit(solution)/shard_map/while/body/eval_jaxpr/psum | solution.py:40
  669.9 24.2 %copy-start.1 = (f32[1024,96]{0,1:T(8,128)S(1)}, f32[1024,96]{0,1:T(8,128)}, u32[]{:S(2)}) copy-start(f32[1024,96]{0,1:T(8,128)} %fusion.101) | copy-start | bytes 1179652 | tf_op jit(solution)/shard_map/while
  693.2 6.2 collective-permute-start
  699.3 28.9 %all-reduce.5.cloned.1.call-start = ((), (), s32[]{:S(2)}) async-start(), calls=%async_computation | async-start | bytes 786432 | tf_op jit(solution)/shard_map/while/body/eval_jaxpr/psum | solution.py:40
  707.6 46.4 %all-reduce.7.cloned.1.call-start = ((), (), s32[]{:S(2)}) async-start(), calls=%async_computation.1 | async-start | bytes 786432 | tf_op jit(solution)/shard_map/while/body/eval_jaxpr/psum | solution.py:40
  733.8 46.2 %all-reduce.9.cloned.1.call-start = ((), (), s32[]{:S(2)}) async-start(), calls=%async_computation.2 | async-start | bytes 786432 | tf_op jit(solution)/shard_map/while/body/eval_jaxpr/psum | solution.py:40
  759.8 45.9 %all-reduce.11.cloned.1.call-start = ((), (), s32[]{:S(2)}) async-start(), calls=%async_computation.3 | async-start | bytes 786432 | tf_op jit(solution)/shard_map/while/body/eval_jaxpr/psum | solution.py:40
  784.3 24.2 %copy-start.1 = (f32[1024,96]{0,1:T(8,128)S(1)}, f32[1024,96]{0,1:T(8,128)}, u32[]{:S(2)}) copy-start(f32[1024,96]{0,1:T(8,128)} %fusion.101) | copy-start | bytes 1179652 | tf_op jit(solution)/shard_map/while
  807.6 6.2 collective-permute-start
  813.7 28.9 %all-reduce.5.cloned.1.call-start = ((), (), s32[]{:S(2)}) async-start(), calls=%async_computation | async-start | bytes 786432 | tf_op jit(solution)/shard_map/while/body/eval_jaxpr/psum | solution.py:40
  822.0 46.4 %all-reduce.7.cloned.1.call-start = ((), (), s32[]{:S(2)}) async-start(), calls=%async_computation.1 | async-start | bytes 786432 | tf_op jit(solution)/shard_map/while/body/eval_jaxpr/psum | solution.py:40
  848.2 46.2 %all-reduce.9.cloned.1.call-start = ((), (), s32[]{:S(2)}) async-start(), calls=%async_computation.2 | async-start | bytes 786432 | tf_op jit(solution)/shard_map/while/body/eval_jaxpr/psum | solution.py:40
  874.2 45.9 %all-reduce.11.cloned.1.call-start = ((), (), s32[]{:S(2)}) async-start(), calls=%async_computation.3 | async-start | bytes 786432 | tf_op jit(solution)/shard_map/while/body/eval_jaxpr/psum | solution.py:40
  898.7 24.2 %copy-start.1 = (f32[1024,96]{0,1:T(8,128)S(1)}, f32[1024,96]{0,1:T(8,128)}, u32[]{:S(2)}) copy-start(f32[1024,96]{0,1:T(8,128)} %fusion.101) | copy-start | bytes 1179652 | tf_op jit(solution)/shard_map/while
  921.9 6.2 collective-permute-start
  (48 other events, 457.1 us)
Sparse Core Ops, SparseCore 0:
  19.1 22.8 all-reduce.4
  47.6 20.0 all-reduce.6
  73.6 19.9 all-reduce.8
  99.4 19.9 all-reduce.10
  135.8 20.4 all-reduce.4
  162.0 20.0 all-reduce.6
  188.0 19.9 all-reduce.8
  213.7 19.9 all-reduce.10
  250.2 20.4 all-reduce.4
  276.4 20.0 all-reduce.6
  302.4 19.9 all-reduce.8
  328.1 19.9 all-reduce.10
  364.6 20.4 all-reduce.4
  390.8 20.0 all-reduce.6
  416.8 19.9 all-reduce.8
  442.5 19.9 all-reduce.10
  479.0 20.4 all-reduce.4
  505.1 20.0 all-reduce.6
  531.2 19.9 all-reduce.8
  556.9 19.9 all-reduce.10
  593.3 20.4 all-reduce.4
  619.5 20.0 all-reduce.6
  645.6 19.9 all-reduce.8
  671.3 19.9 all-reduce.10
  707.7 20.4 all-reduce.4
  733.9 20.0 all-reduce.6
  759.9 19.9 all-reduce.8
  785.7 19.9 all-reduce.10
  822.1 20.4 all-reduce.4
  848.3 20.0 all-reduce.6
  874.3 19.9 all-reduce.8
  900.1 19.9 all-reduce.10
where the time goes:
time: 939 us; the launch traced here: 936 us
  waiting for transfers between devices  625 us (67%)
  matrix products  216 us (23%)
  other arithmetic  65.5 us (7%)
  between operations  13.7 us (1%)
    psum x32, waiting for transfers between devices, sub_epoch(): grad_item = lax.psum(part_item, 'sub') + decay_coef * item_st  595 us
    dot_general x32, matrix products, sub_epoch(): lax.dot_general(user_half, item_half, (((1,), (1,)), ((), ())), preferred...  102 us
    dot_general x32, matrix products, sub_epoch(): jnp.dot(err_half, item_half, preferred_element_type=jnp.float32)  67.4 us
    dot_general x32, matrix products, sub_epoch(): lax.dot_general(err_half, user_half, (((0,), (0,)), ((), ())), preferred_...  47.2 us
    ppermute x8, waiting for transfers between devices, sub_epoch(): return (user_st, lax.ppermute(item_st, 'blk', prev_pairs))  29.9 us
    sub x16, other arithmetic, sub_epoch(): item_st = item_st - step_size * grad_item  25.6 us
    ne x8, other arithmetic, sub_epoch(): mask_now = lax.dynamic_slice_in_dim(mask, col_start, items_dev, axis=1) != 0  22 us
  transfers between devices with their start and end apart: 40, of which 40 were waited for; matrix products, arithmetic and copies ran while one was open for 7% of the time, Pallas kernels for 0%

commit v1 on v0

v1 whole, which is shorter than its diff:
```python
import functools
import math

import jax
import jax.numpy as jnp
from jax import lax
from jax.experimental import pallas as pl
from jax.experimental.pallas import tpu as pltpu
from jax.sharding import PartitionSpec as P

STEPS = 4
EPOCHS = 2
STEP_GAIN = 0.4
DECAY = 0.002
CHUNK = 128
ROWS = 256
MESH = pl.DeviceIdType.MESH
NT = (((1,), (1,)), ((), ()))


def run(n_blk, eta, lam, r_hbm, m_hbm, u_hbm, v_hbm, u_out, v_out,
        rate, known, err, users, users_bf, users_t, own, own_bf, own_next, part, send_p, recv_p,
        peer_v, in_v, last_v, v_start, edge_f, edge_b,
        load_sem, uv_sem, p_send, p_recv, v_send, v_recv,
        ef_send, ef_recv, eb_send, eb_recv, el_send, el_recv):
    rank, n_users = users.shape
    half = own.shape[1]
    n_chunks = half // CHUNK
    n_sub_epochs = EPOCHS * n_blk
    pad = users_bf.shape[1] - rank
    me = lax.axis_index('sub')
    other = 1 - me
    blk = lax.axis_index('blk')
    down = lax.rem(blk + n_blk - 1, n_blk)
    up = lax.rem(blk + 1, n_blk)

    def load(t, role):
        owner = me if role else other
        col = pl.multiple_of(lax.rem(blk + t, n_blk) * (2 * half) + owner * half, half)
        return [
            pltpu.make_async_copy(src.at[:, pl.ds(col, half)], dst.at[t, role], load_sem.at[t, role, j])
            for j, (src, dst) in enumerate(((r_hbm, rate), (m_hbm, known)))
        ]

    def start_load(t):
        for role in range(2):
            for copy in load(t, role):
                copy.start()

    u_copy = pltpu.make_async_copy(u_hbm, users, uv_sem.at[0])
    v_copy = pltpu.make_async_copy(v_hbm, v_start, uv_sem.at[1])
    u_copy.start()
    v_copy.start()
    start_load(0)

    barrier = pltpu.get_barrier_semaphore()
    friends = [(blk, other), (down, me), (down, other), (up, me), (up, other)]
    for b, s in friends:
        pl.semaphore_signal(barrier, inc=1, device_id={'sub': s, 'blk': b}, device_id_type=MESH)

    def refresh_users(u):
        u_bf = u.astype(jnp.bfloat16)
        users_t[...] = u_bf
        wide = jnp.concatenate([u, jnp.zeros((pad, n_users), jnp.float32)], axis=0)
        users_bf[...] = wide.T.astype(jnp.bfloat16)

    u_copy.wait()
    refresh_users(users[...])
    v_copy.wait()
    for c in range(n_chunks):
        mine = pl.ds(pl.multiple_of(me * half + c * CHUNK, CHUNK), CHUNK)
        theirs = pl.ds(pl.multiple_of(other * half + c * CHUNK, CHUNK), CHUNK)
        in_v[0, c] = v_start[:, mine]
        peer_v[0, c] = v_start[:, theirs].astype(jnp.bfloat16)
    pl.semaphore_wait(barrier, len(friends))

    def remote(src, dst, send, recv, s, b):
        return pltpu.make_async_remote_copy(
            src_ref=src, dst_ref=dst, send_sem=send, recv_sem=recv,
            device_id={'sub': s, 'blk': b}, device_id_type=MESH)

    def part_copy(k, slot, c):
        return remote(send_p.at[slot, c], recv_p.at[k, c], p_send.at[slot, c], p_recv.at[slot, c], other, blk)

    def item_copy(k, q, c):
        return remote(own_next.at[q, c], peer_v.at[k + 1, c], v_send.at[q, c], v_recv.at[c], other, blk)

    def edge_own(t, c):
        slot = lax.rem(t, 2)
        return remote(edge_f.at[slot, c], in_v.at[t + 1, c], ef_send.at[slot, c], ef_recv.at[t, c], me, down)

    def edge_peer(t, c):
        slot = lax.rem(t, 2)
        return remote(edge_b.at[slot, c], peer_v.at[STEPS * (t + 1), c], eb_send.at[slot, c], eb_recv.at[t, c], other, down)

    def edge_last(t, c):
        slot = lax.rem(t, 2)
        return remote(edge_f.at[slot, c], last_v.at[c], el_send.at[c], el_recv.at[c], other, down)

    def widen(v):
        return jnp.concatenate([v, jnp.zeros((pad, v.shape[1]), v.dtype)], axis=0)

    def errors(tm, role, cols, v_bf):
        v_wide = widen(v_bf)
        for r in range(0, n_users, ROWS):
            rows = pl.ds(r, ROWS)
            pred = jnp.dot(users_bf[rows, :], v_wide, preferred_element_type=jnp.float32)
            diff = jnp.where(known[tm, role, rows, cols] != 0, pred - rate[tm, role, rows, cols], 0.0)
            err[role, rows, cols] = diff.astype(jnp.bfloat16)

    def sub_epoch(t, carry):
        tm = lax.rem(t, n_blk)
        for q in range(STEPS):
            k = STEPS * t + q
            slot = q % 2
            if q == 0:
                @pl.when(t < n_blk)
                def _():
                    for copy in load(t, 0):
                        copy.wait()
            for c in range(n_chunks):
                if q == 0:
                    @pl.when(t > 0)
                    def _():
                        edge_peer(t - 1, c).wait_recv()
                else:
                    item_copy(k - 1, q - 1, c).wait_recv()
                cols = pl.ds(c * CHUNK, CHUNK)
                errors(tm, 0, cols, peer_v[k, c])
                total = jnp.dot(users_t[...], err[0, :, cols], preferred_element_type=jnp.float32)
                if q < 2:
                    @pl.when(t > 0)
                    def _():
                        part_copy(k - 2, slot, c).wait_send()
                else:
                    part_copy(k - 2, slot, c).wait_send()
                send_p[slot, c] = total
                part_copy(k, slot, c).start()
            if q == 0:
                @pl.when(t + 1 < n_blk)
                def _():
                    start_load(t + 1)

                @pl.when(t < n_blk)
                def _():
                    for copy in load(t, 1):
                        copy.wait()
                for c in range(n_chunks):
                    @pl.when(t > 0)
                    def _():
                        edge_own(t - 1, c).wait_recv()
                    v = in_v[t, c]
                    own[:, pl.ds(c * CHUNK, CHUNK)] = v
                    own_bf[:, pl.ds(c * CHUNK, CHUNK)] = v.astype(jnp.bfloat16)
            for c in range(0, half, 256):
                cols = pl.ds(c, 256)
                errors(tm, 1, cols, own_bf[:, cols])
                part[:, cols] = jnp.dot(users_t[...], err[1, :, cols], preferred_element_type=jnp.float32)
            v_peer = jnp.concatenate([peer_v[k, c] for c in range(n_chunks)], axis=1)
            v_own = own_bf[...]
            for r in range(0, n_users, ROWS):
                rows = pl.ds(r, ROWS)
                grad = lax.dot_general(v_peer, err[0, rows, :], NT, preferred_element_type=jnp.float32)
                grad += lax.dot_general(v_own, err[1, rows, :], NT, preferred_element_type=jnp.float32)
                u = users[:, rows]
                users[:, rows] = u - eta * (grad + lam * u)
            refresh_users(users[...])
            for c in range(n_chunks):
                cols = pl.ds(c * CHUNK, CHUNK)
                part_copy(k, slot, c).wait_recv()
                v = own[:, cols]
                v = v - eta * ((part[:, cols] + recv_p[k, c]) + lam * v)
                if q < STEPS - 1:
                    own[:, cols] = v
                    v_bf = v.astype(jnp.bfloat16)
                    own_bf[:, cols] = v_bf

                    @pl.when(t > 0)
                    def _():
                        item_copy(k - STEPS, q, c).wait_send()
                    own_next[q, c] = v_bf
                    item_copy(k, q, c).start()
                else:
                    @pl.when(t > 1)
                    def _():
                        edge_own(t - 2, c).wait_send()
                        edge_peer(t - 2, c).wait_send()
                    edge_slot = lax.rem(t, 2)
                    edge_f[edge_slot, c] = v
                    edge_b[edge_slot, c] = v.astype(jnp.bfloat16)

                    @pl.when(t < n_sub_epochs - 1)
                    def _():
                        edge_peer(t, c).start()

                    @pl.when(t == n_sub_epochs - 1)
                    def _():
                        edge_last(t, c).start()
                    edge_own(t, c).start()
        return carry

    lax.fori_loop(0, n_sub_epochs, sub_epoch, 0)

    u_back = pltpu.make_async_copy(users, u_out, uv_sem.at[0])
    u_back.start()
    end = n_sub_epochs - 1
    last_k = STEPS * n_sub_epochs - 1
    for c in range(n_chunks):
        mine = pl.ds(pl.multiple_of(me * half + c * CHUNK, CHUNK), CHUNK)
        theirs = pl.ds(pl.multiple_of(other * half + c * CHUNK, CHUNK), CHUNK)
        edge_own(end, c).wait_recv()
        v_start[:, mine] = in_v[n_sub_epochs, c]
        edge_last(end, c).wait_recv()
        v_start[:, theirs] = last_v[c]
    v_back = pltpu.make_async_copy(v_start, v_out, uv_sem.at[1])
    v_back.start()
    for c in range(n_chunks):
        part_copy(last_k - 1, 0, c).wait_send()
        part_copy(last_k, 1, c).wait_send()
        for q in range(STEPS - 1):
            item_copy(STEPS * end + q, q, c).wait_send()
        edge_own(end - 1, c).wait_send()
        edge_peer(end - 1, c).wait_send()
        edge_own(end, c).wait_send()
        edge_last(end, c).wait_send()
    u_back.wait()
    v_back.wait()


def solution(mesh):
    n_blk = mesh.shape['blk']
    n_sub = mesh.shape['sub']
    row_spec = P(('rep', 'blk', 'sub'), None)
    item_spec = P(('rep', 'blk'), None)

    def local_run(ratings, mask, user_init, item_init):
        n_users = ratings.shape[0]
        n_items, rank = item_init.shape
        half = n_items // n_sub
        n_chunks = half // CHUNK
        n_sub_epochs = EPOCHS * n_blk
        n_steps = STEPS * n_sub_epochs
        wide = 128
        big_side = max(n_items, n_sub * n_users)
        eta = STEP_GAIN * math.sqrt(rank) / (math.sqrt(big_side) + math.sqrt(rank)) ** 2
        lam = DECAY / eta
        f32, bf16 = jnp.float32, jnp.bfloat16
        dma = pltpu.SemaphoreType.DMA
        chunk = (rank, CHUNK)
        any_space = pl.BlockSpec(memory_space=pl.ANY)
        users_t, items_t = pl.pallas_call(
            functools.partial(run, n_blk, eta, lam),
            out_shape=[jax.ShapeDtypeStruct((rank, n_users), f32), jax.ShapeDtypeStruct((rank, n_items), f32)],
            in_specs=[any_space] * 4,
            out_specs=[any_space] * 2,
            scratch_shapes=[
                pltpu.VMEM((n_blk, 2, n_users, half), f32),
                pltpu.VMEM((n_blk, 2, n_users, half), jnp.int32),
                pltpu.VMEM((2, n_users, half), bf16),
                pltpu.VMEM((rank, n_users), f32),
                pltpu.VMEM((n_users, wide), bf16),
                pltpu.VMEM((rank, n_users), bf16),
                pltpu.VMEM((rank, half), f32),
                pltpu.VMEM((rank, half), bf16),
                pltpu.VMEM((STEPS - 1, n_chunks) + chunk, bf16),
                pltpu.VMEM((rank, half), f32),
                pltpu.VMEM((2, n_chunks) + chunk, f32),
                pltpu.VMEM((n_steps, n_chunks) + chunk, f32),
                pltpu.VMEM((n_steps + 1, n_chunks) + chunk, bf16),
                pltpu.VMEM((n_sub_epochs + 1, n_chunks) + chunk, f32),
                pltpu.VMEM((n_chunks,) + chunk, f32),
                pltpu.VMEM((rank, n_items), f32),
                pltpu.VMEM((2, n_chunks) + chunk, f32),
                pltpu.VMEM((2, n_chunks) + chunk, bf16),
                dma((n_blk, 2, 2)),
                dma((2,)),
                dma((2, n_chunks)),
                dma((2, n_chunks)),
                dma((STEPS - 1, n_chunks)),
                dma((n_chunks,)),
                dma((2, n_chunks)),
                dma((n_sub_epochs, n_chunks)),
                dma((2, n_chunks)),
                dma((n_sub_epochs, n_chunks)),
                dma((n_chunks,)),
                dma((n_chunks,)),
            ],
            compiler_params=pltpu.CompilerParams(
                collective_id=0, has_side_effects=True, vmem_limit_bytes=64_000_000),
        )(ratings, mask, user_init.T, item_init.T)
        return users_t.T, items_t.T

    return jax.shard_map(local_run, mesh=mesh, in_specs=(row_spec, row_spec, row_spec, item_spec), out_specs=(row_spec, item_spec), check_vma=False)
```

time: 939 us -> 251 us (0.27)
  waiting for transfers between devices: 625 us -> 0 us
  Pallas kernels: 0 us -> 245 us
  matrix products: 216 us -> 0 us
  other arithmetic: 65.5 us -> 0 us
  between operations: 13.7 us -> 0.64 us
    psum x32 -> x0, waiting for transfers between devices: 595 us -> none  [sub_epoch(): grad_item = lax.psum(part_item, 'sub') + decay_coef * item_st]
    pallas_call x0 -> x1, Pallas kernels: none -> 245 us  [local_run(): pl.pallas_call(functools.partial(run, n_blk, eta, lam), out_shape=[jax.Sh...]
    dot_general x96 -> x0, matrix products: 216 us -> none  [the longest x32 102 us: sub_epoch(): lax.dot_general(user_half, item_half, (((1,), (1,)), ((), ())), preferred...]
    ppermute x8 -> x0, waiting for transfers between devices: 29.9 us -> none  [sub_epoch(): return (user_st, lax.ppermute(item_st, 'blk', prev_pairs))]
    sub x16 -> x0, other arithmetic: 25.6 us -> none  [sub_epoch(): item_st = item_st - step_size * grad_item]
    ne x8 -> x0, other arithmetic: 22 us -> none  [sub_epoch(): mask_now = lax.dynamic_slice_in_dim(mask, col_start, items_dev, axis=1) != 0]
    convert_element_type x16 -> x0, other arithmetic: 18 us -> none  [sub_epoch(): item_half = item_st.astype(jnp.bfloat16)]
  transfers between devices with their start and end apart: 40 -> 0, of which waited for: 40 -> 0; matrix products, arithmetic and copies ran while one was open for 7% -> 0% of each run, Pallas kernels for 0% -> 0%
where the time goes in v1:
time: 251 us; the launch traced here: 249 us
  Pallas kernels  245 us (98%)
  local copies, waits for them, and re-layouts  3.53 us (1%)
    pallas_call x1, Pallas kernels, local_run(): pl.pallas_call(functools.partial(run, n_blk, eta, lam), out_shape=[jax.Sh...  245 us

profile of v1, /device:TPU:0, one launch (start us, length us, event | category | flops | bytes accessed | tf_op | source)
XLA Modules:
  0.0 249.4 jit_solution(6884944116434358586)
XLA Ops:
  0.6 245.2 %shard_map.59 = (f32[96,1024]{1,0:T(8,128)}, f32[96,1024]{1,0:T(8,128)}) custom-call(f32[1024,4096]{1,0:T(8,128)} %r_hbm.1, s32[1024,4096]{1,0:T(8,128)} %m_hbm.1, f32[96,1024]{1,0:T(8,128)} %bitcast.4, f32[96,1024]{1,0:T(8,128)} %bitcast.5), custom_call_target="tpu_custom_call" | custom-call | tf_op jit(solution)/shard_map/pallas_call | solution.py:251
  245.8 1.8 copy.8
  247.6 1.8 copy.9

commit v2 on v1

--- a/solution.py
+++ b/solution.py
@@ -14,6 +14,7 @@
 DECAY = 0.002
 CHUNK = 128
 ROWS = 256
+PIECES = 2
 MESH = pl.DeviceIdType.MESH
 NT = (((1,), (1,)), ((), ()))
 
@@ -79,11 +80,15 @@
             src_ref=src, dst_ref=dst, send_sem=send, recv_sem=recv,
             device_id={'sub': s, 'blk': b}, device_id_type=MESH)
 
-    def part_copy(k, slot, c):
-        return remote(send_p.at[slot, c], recv_p.at[k, c], p_send.at[slot, c], p_recv.at[slot, c], other, blk)
-
-    def item_copy(k, q, c):
-        return remote(own_next.at[q, c], peer_v.at[k + 1, c], v_send.at[q, c], v_recv.at[c], other, blk)
+    piece = rank // PIECES
+
+    def part_copy(k, slot, c, p):
+        at = pl.ds(p * piece, piece)
+        return remote(send_p.at[slot, c, at], recv_p.at[k, c, at], p_send.at[slot, c, p], p_recv.at[slot, c, p], other, blk)
+
+    def item_copy(k, q, c, p):
+        at = pl.ds(p * piece, piece)
+        return remote(own_next.at[q, c, at], peer_v.at[k + 1, c, at], v_send.at[q, c, p], v_recv.at[c, p], other, blk)
 
     def edge_own(t, c):
         slot = lax.rem(t, 2)
@@ -124,18 +129,21 @@
                     def _():
                         edge_peer(t - 1, c).wait_recv()
                 else:
-                    item_copy(k - 1, q - 1, c).wait_recv()
+                    for p in range(PIECES):
+                        item_copy(k - 1, q - 1, c, p).wait_recv()
                 cols = pl.ds(c * CHUNK, CHUNK)
                 errors(tm, 0, cols, peer_v[k, c])
                 total = jnp.dot(users_t[...], err[0, :, cols], preferred_element_type=jnp.float32)
-                if q < 2:
-                    @pl.when(t > 0)
-                    def _():
-                        part_copy(k - 2, slot, c).wait_send()
-                else:
-                    part_copy(k - 2, slot, c).wait_send()
+                for p in range(PIECES):
+                    if q < 2:
+                        @pl.when(t > 0)
+                        def _():
+                            part_copy(k - 2, slot, c, p).wait_send()
+                    else:
+                        part_copy(k - 2, slot, c, p).wait_send()
                 send_p[slot, c] = total
-                part_copy(k, slot, c).start()
+                for p in range(PIECES):
+                    part_copy(k, slot, c, p).start()
             if q == 0:
                 @pl.when(t + 1 < n_blk)
                 def _():
@@ -167,28 +175,32 @@
             refresh_users(users[...])
             for c in range(n_chunks):
                 cols = pl.ds(c * CHUNK, CHUNK)
-                part_copy(k, slot, c).wait_recv()
-                v = own[:, cols]
-                v = v - eta * ((part[:, cols] + recv_p[k, c]) + lam * v)
                 if q < STEPS - 1:
-                    own[:, cols] = v
-                    v_bf = v.astype(jnp.bfloat16)
-                    own_bf[:, cols] = v_bf
-
                     @pl.when(t > 0)
                     def _():
-                        item_copy(k - STEPS, q, c).wait_send()
-                    own_next[q, c] = v_bf
-                    item_copy(k, q, c).start()
+                        for p in range(PIECES):
+                            item_copy(k - STEPS, q, c, p).wait_send()
                 else:
                     @pl.when(t > 1)
                     def _():
                         edge_own(t - 2, c).wait_send()
                         edge_peer(t - 2, c).wait_send()
-                    edge_slot = lax.rem(t, 2)
-                    edge_f[edge_slot, c] = v
-                    edge_b[edge_slot, c] = v.astype(jnp.bfloat16)
-
+                for p in range(PIECES):
+                    at = pl.ds(p * piece, piece)
+                    part_copy(k, slot, c, p).wait_recv()
+                    v = own[at, cols]
+                    v = v - eta * ((part[at, cols] + recv_p[k, c, at]) + lam * v)
+                    v_bf = v.astype(jnp.bfloat16)
+                    if q < STEPS - 1:
+                        own_next[q, c, at] = v_bf
+                        item_copy(k, q, c, p).start()
+                        own[at, cols] = v
+                        own_bf[at, cols] = v_bf
+                    else:
+                        edge_slot = lax.rem(t, 2)
+                        edge_f[edge_slot, c, at] = v
+                        edge_b[edge_slot, c, at] = v_bf
+                if q == STEPS - 1:
                     @pl.when(t < n_sub_epochs - 1)
                     def _():
                         edge_peer(t, c).start()
@@ -215,10 +227,11 @@
     v_back = pltpu.make_async_copy(v_start, v_out, uv_sem.at[1])
     v_back.start()
     for c in range(n_chunks):
-        part_copy(last_k - 1, 0, c).wait_send()
-        part_copy(last_k, 1, c).wait_send()
-        for q in range(STEPS - 1):
-            item_copy(STEPS * end + q, q, c).wait_send()
+        for p in range(PIECES):
+            part_copy(last_k - 1, 0, c, p).wait_send()
+            part_copy(last_k, 1, c, p).wait_send()
+            for q in range(STEPS - 1):
+                item_copy(STEPS * end + q, q, c, p).wait_send()
         edge_own(end - 1, c).wait_send()
         edge_peer(end - 1, c).wait_send()
         edge_own(end, c).wait_send()
@@ -274,10 +287,10 @@
                 pltpu.VMEM((2, n_chunks) + chunk, bf16),
                 dma((n_blk, 2, 2)),
                 dma((2,)),
-                dma((2, n_chunks)),
-                dma((2, n_chunks)),
-                dma((STEPS - 1, n_chunks)),
-                dma((n_chunks,)),
+                dma((2, n_chunks, PIECES)),
+                dma((2, n_chunks, PIECES)),
+                dma((STEPS - 1, n_chunks, PIECES)),
+                dma((n_chunks, PIECES)),
                 dma((2, n_chunks)),
                 dma((n_sub_epochs, n_chunks)),
                 dma((2, n_chunks)),

time: 251 us -> 249 us (level)
  no operation moved by 1% of the time
where the time goes in v2:
time: 249 us; the launch traced here: 248 us
  Pallas kernels  244 us (98%)
  local copies, waits for them, and re-layouts  3.53 us (1%)
    pallas_call x1, Pallas kernels, local_run(): pl.pallas_call(functools.partial(run, n_blk, eta, lam), out_shape=[jax.Sh...  244 us

profile of v2, /device:TPU:0, one launch (start us, length us, event | category | flops | bytes accessed | tf_op | source)
XLA Modules:
  0.0 247.9 jit_solution(12296378284819986398)
XLA Ops:
  0.6 243.7 %shard_map.59 = (f32[96,1024]{1,0:T(8,128)}, f32[96,1024]{1,0:T(8,128)}) custom-call(f32[1024,4096]{1,0:T(8,128)} %r_hbm.1, s32[1024,4096]{1,0:T(8,128)} %m_hbm.1, f32[96,1024]{1,0:T(8,128)} %bitcast.4, f32[96,1024]{1,0:T(8,128)} %bitcast.5), custom_call_target="tpu_custom_call" | custom-call | tf_op jit(solution)/shard_map/pallas_call | solution.py:264
  244.3 1.8 copy.8
  246.1 1.8 copy.9

commit v3 on v2

v3 whole, which is shorter than its diff:
```python
import functools
import math

import jax
import jax.numpy as jnp
from jax import lax
from jax.experimental import pallas as pl
from jax.experimental.pallas import tpu as pltpu
from jax.sharding import PartitionSpec as P

STEPS = 4
EPOCHS = 2
STEP_GAIN = 0.4
DECAY = 0.002
CHUNK = 128
ROWS = 256
PIECES = 2
ORDERS = (
    ('A0', 'A1', 'A2', 'A3', 'B', 'C0', 'M', 'C1', 'C2', 'C3'),
    ('A0', 'A1', 'D2', 'D3', 'B', 'C0', 'A2', 'C1', 'A3', 'M'),
)
MESH = pl.DeviceIdType.MESH
NT = (((1,), (1,)), ((), ()))


def run(n_blk, eta, lam, r_hbm, m_hbm, u_hbm, v_hbm, u_out, v_out,
        rate, known, err, users, users_bf, users_t, own, own_bf, own_next, part, send_p, recv_p,
        peer_v, in_v, v_start, edge_f, edge_b,
        load_sem, uv_sem, p_send, p_recv, v_send, v_recv,
        ef_send, ef_recv, eb_send, eb_recv, el_send, el_recv):
    rank, n_users = users.shape
    half = own.shape[1]
    n_chunks = half // CHUNK
    n_sub_epochs = EPOCHS * n_blk
    pad = users_bf.shape[1] - rank
    me = lax.axis_index('sub')
    other = 1 - me
    blk = lax.axis_index('blk')
    down = lax.rem(blk + n_blk - 1, n_blk)
    up = lax.rem(blk + 1, n_blk)

    def load(t, role):
        owner = me if role else other
        col = pl.multiple_of(lax.rem(blk + t, n_blk) * (2 * half) + owner * half, half)
        return [
            pltpu.make_async_copy(src.at[:, pl.ds(col, half)], dst.at[t, role], load_sem.at[t, role, j])
            for j, (src, dst) in enumerate(((r_hbm, rate), (m_hbm, known)))
        ]

    def start_load(t):
        for role in range(2):
            for copy in load(t, role):
                copy.start()

    u_copy = pltpu.make_async_copy(u_hbm, users, uv_sem.at[0])
    v_copy = pltpu.make_async_copy(v_hbm, v_start, uv_sem.at[1])
    u_copy.start()
    v_copy.start()
    for copy in load(0, 0):
        copy.start()

    barrier = pltpu.get_barrier_semaphore()
    friends = [(blk, other), (down, me), (down, other), (up, me), (up, other)]
    for b, s in friends:
        pl.semaphore_signal(barrier, inc=1, device_id={'sub': s, 'blk': b}, device_id_type=MESH)

    def refresh_users(u):
        u_bf = u.astype(jnp.bfloat16)
        users_t[...] = u_bf
        wide = jnp.concatenate([u, jnp.zeros((pad, n_users), jnp.float32)], axis=0)
        users_bf[...] = wide.T.astype(jnp.bfloat16)

    u_copy.wait()
    refresh_users(users[...])
    v_copy.wait()

    def mine(c):
        return pl.ds(pl.multiple_of(me * half + c * CHUNK, CHUNK), CHUNK)

    for c in range(n_chunks):
        theirs = pl.ds(pl.multiple_of(other * half + c * CHUNK, CHUNK), CHUNK)
        in_v[0, c] = v_start[:, mine(c)]
        peer_v[0, c] = v_start[:, theirs].astype(jnp.bfloat16)
    for copy in load(0, 0):
        copy.wait()
    for copy in load(0, 1):
        copy.start()
    pl.semaphore_wait(barrier, len(friends))

    def remote(src, dst, send, recv, s, b):
        return pltpu.make_async_remote_copy(
            src_ref=src, dst_ref=dst, send_sem=send, recv_sem=recv,
            device_id={'sub': s, 'blk': b}, device_id_type=MESH)

    piece = rank // PIECES

    def part_copy(k, slot, c, p):
        at = pl.ds(p * piece, piece)
        return remote(send_p.at[slot, c, at], recv_p.at[k, c, at], p_send.at[slot, c, p], p_recv.at[slot, c, p], other, blk)

    def item_copy(k, q, c, p):
        at = pl.ds(p * piece, piece)
        return remote(own_next.at[q, c, at], peer_v.at[k + 1, c, at], v_send.at[q, c, p], v_recv.at[c, p], other, blk)

    def edge_own(t, c):
        slot = lax.rem(t, 2)
        return remote(edge_f.at[slot, c], in_v.at[t + 1, c], ef_send.at[slot, c], ef_recv.at[t, c], me, down)

    def edge_peer(t, c):
        slot = lax.rem(t, 2)
        return remote(edge_b.at[slot, c], peer_v.at[STEPS * (t + 1), c], eb_send.at[slot, c], eb_recv.at[t, c], other, down)

    def edge_last(t, c):
        slot = lax.rem(t, 2)
        return remote(edge_f.at[slot, c], v_out.at[:, mine(c)], el_send.at[c], el_recv.at[c], other, down)

    def edge_end(t, c):
        slot = lax.rem(t, 2)
        return remote(edge_f.at[slot, c], v_out.at[:, mine(c)], ef_send.at[slot, c], ef_recv.at[t, c], me, down)

    def widen(v):
        return jnp.concatenate([v, jnp.zeros((pad, v.shape[1]), v.dtype)], axis=0)

    def errors(tm, role, cols, v_bf):
        v_wide = widen(v_bf)
        for r in range(0, n_users, ROWS):
            rows = pl.ds(r, ROWS)
            pred = jnp.dot(users_bf[rows, :], v_wide, preferred_element_type=jnp.float32)
            diff = jnp.where(known[tm, role, rows, cols] != 0, pred - rate[tm, role, rows, cols], 0.0)
            err[role, rows, cols] = diff.astype(jnp.bfloat16)

    def send_part(t, q, c):
        k, slot = STEPS * t + q, q % 2
        if q == 0:
            @pl.when(t > 0)
            def _():
                edge_peer(t - 1, c).wait_recv()
        else:
            for p in range(PIECES):
                item_copy(k - 1, q - 1, c, p).wait_recv()
        cols = pl.ds(c * CHUNK, CHUNK)
        errors(lax.rem(t, n_blk), 0, cols, peer_v[k, c])
        total = jnp.dot(users_t[...], err[0, :, cols], preferred_element_type=jnp.float32)
        for p in range(PIECES):
            if q < 2:
                @pl.when(t > 0)
                def _():
                    part_copy(k - 2, slot, c, p).wait_send()
            else:
                part_copy(k - 2, slot, c, p).wait_send()
        send_p[slot, c] = total
        for p in range(PIECES):
            part_copy(k, slot, c, p).start()

    def own_part(t, q):
        if q == 0:
            @pl.when(t + 1 < n_blk)
            def _():
                start_load(t + 1)

            @pl.when(t < n_blk)
            def _():
                for copy in load(t, 1):
                    copy.wait()
            for c in range(n_chunks):
                @pl.when(t > 0)
                def _():
                    edge_own(t - 1, c).wait_recv()
                v = in_v[t, c]
                own[:, pl.ds(c * CHUNK, CHUNK)] = v
                own_bf[0, :, pl.ds(c * CHUNK, CHUNK)] = v.astype(jnp.bfloat16)
        for c in range(0, half, 256):
            cols = pl.ds(c, 256)
            errors(lax.rem(t, n_blk), 1, cols, own_bf[q % 2, :, cols])
            part[:, cols] = jnp.dot(users_t[...], err[1, :, cols], preferred_element_type=jnp.float32)

    def step_users(t, q):
        k = STEPS * t + q
        v_peer = jnp.concatenate([peer_v[k, c] for c in range(n_chunks)], axis=1)
        v_own = own_bf[q % 2]
        for r in range(0, n_users, ROWS):
            rows = pl.ds(r, ROWS)
            grad = lax.dot_general(v_peer, err[0, rows, :], NT, preferred_element_type=jnp.float32)
            grad += lax.dot_general(v_own, err[1, rows, :], NT, preferred_element_type=jnp.float32)
            u = users[:, rows]
            users[:, rows] = u - eta * (grad + lam * u)
        refresh_users(users[...])

    def step_items(t, q, c):
        k, slot = STEPS * t + q, q % 2
        cols = pl.ds(c * CHUNK, CHUNK)
        edge_slot = lax.rem(t, 2)
        if q < STEPS - 1:
            @pl.when(t > 0)
            def _():
                for p in range(PIECES):
                    item_copy(k - STEPS, q, c, p).wait_send()
        else:
            @pl.when(t > 1)
            def _():
                edge_own(t - 2, c).wait_send()
                edge_peer(t - 2, c).wait_send()
        for p in range(PIECES):
            at = pl.ds(p * piece, piece)
            part_copy(k, slot, c, p).wait_recv()
            v = own[at, cols]
            v = v - eta * ((part[at, cols] + recv_p[k, c, at]) + lam * v)
            v_bf = v.astype(jnp.bfloat16)
            if q < STEPS - 1:
                own_next[q, c, at] = v_bf
                item_copy(k, q, c, p).start()
                own[at, cols] = v
                own_bf[(q + 1) % 2, at, cols] = v_bf
            else:
                edge_f[edge_slot, c, at] = v
                edge_b[edge_slot, c, at] = v_bf
        if q == STEPS - 1:
            @pl.when(t < n_sub_epochs - 1)
            def _():
                edge_peer(t, c).start()
                edge_own(t, c).start()

            @pl.when(t == n_sub_epochs - 1)
            def _():
                edge_last(t, c).start()
                edge_end(t, c).start()

    def sub_epoch(t, carry):
        @pl.when((t > 0) & (t < n_blk))
        def _():
            for copy in load(t, 0):
                copy.wait()
        for core, order in enumerate(ORDERS):
            @pl.when(lax.rem(blk, 2) == core)
            def _():
                for q in range(STEPS):
                    for op in order:
                        c = int(op[1:] or 0)
                        if op[0] == 'A':
                            send_part(t, q, c)
                        elif op[0] == 'D' and q > 0:
                            step_items(t, q - 1, c)
                        elif op[0] == 'B':
                            own_part(t, q)
                        elif op[0] == 'C':
                            step_items(t, q, c)
                        elif op[0] == 'M':
                            step_users(t, q)
                for op in order:
                    if op[0] == 'D':
                        step_items(t, STEPS - 1, int(op[1:]))
        return carry

    lax.fori_loop(0, n_sub_epochs, sub_epoch, 0)

    u_back = pltpu.make_async_copy(users, u_out, uv_sem.at[0])
    u_back.start()
    end = n_sub_epochs - 1
    last_k = STEPS * n_sub_epochs - 1
    for c in range(n_chunks):
        edge_end(end, c).wait_recv()
        edge_last(end, c).wait_recv()
    for c in range(n_chunks):
        for p in range(PIECES):
            part_copy(last_k - 1, 0, c, p).wait_send()
            part_copy(last_k, 1, c, p).wait_send()
            for q in range(STEPS - 1):
                item_copy(STEPS * end + q, q, c, p).wait_send()
        edge_own(end - 1, c).wait_send()
        edge_peer(end - 1, c).wait_send()
        edge_end(end, c).wait_send()
        edge_last(end, c).wait_send()
    u_back.wait()


def solution(mesh):
    n_blk = mesh.shape['blk']
    n_sub = mesh.shape['sub']
    row_spec = P(('rep', 'blk', 'sub'), None)
    item_spec = P(('rep', 'blk'), None)

    def local_run(ratings, mask, user_init, item_init):
        n_users = ratings.shape[0]
        n_items, rank = item_init.shape
        half = n_items // n_sub
        n_chunks = half // CHUNK
        n_sub_epochs = EPOCHS * n_blk
        n_steps = STEPS * n_sub_epochs
        wide = 128
        big_side = max(n_items, n_sub * n_users)
        eta = STEP_GAIN * math.sqrt(rank) / (math.sqrt(big_side) + math.sqrt(rank)) ** 2
        lam = DECAY / eta
        f32, bf16 = jnp.float32, jnp.bfloat16
        dma = pltpu.SemaphoreType.DMA
        chunk = (rank, CHUNK)
        any_space = pl.BlockSpec(memory_space=pl.ANY)
        users_t, items_t = pl.pallas_call(
            functools.partial(run, n_blk, eta, lam),
            out_shape=[jax.ShapeDtypeStruct((rank, n_users), f32), jax.ShapeDtypeStruct((rank, n_items), f32)],
            in_specs=[any_space] * 4,
            out_specs=[any_space] * 2,
            scratch_shapes=[
                pltpu.VMEM((n_blk, 2, n_users, half), f32),
                pltpu.VMEM((n_blk, 2, n_users, half), jnp.int32),
                pltpu.VMEM((2, n_users, half), bf16),
                pltpu.VMEM((rank, n_users), f32),
                pltpu.VMEM((n_users, wide), bf16),
                pltpu.VMEM((rank, n_users), bf16),
                pltpu.VMEM((rank, half), f32),
                pltpu.VMEM((2, rank, half), bf16),
                pltpu.VMEM((STEPS - 1, n_chunks) + chunk, bf16),
                pltpu.VMEM((rank, half), f32),
                pltpu.VMEM((2, n_chunks) + chunk, f32),
                pltpu.VMEM((n_steps, n_chunks) + chunk, f32),
                pltpu.VMEM((n_steps + 1, n_chunks) + chunk, bf16),
                pltpu.VMEM((n_sub_epochs, n_chunks) + chunk, f32),
                pltpu.VMEM((rank, n_items), f32),
                pltpu.VMEM((2, n_chunks) + chunk, f32),
                pltpu.VMEM((2, n_chunks) + chunk, bf16),
                dma((n_blk, 2, 2)),
                dma((2,)),
                dma((2, n_chunks, PIECES)),
                dma((2, n_chunks, PIECES)),
                dma((STEPS - 1, n_chunks, PIECES)),
                dma((n_chunks, PIECES)),
                dma((2, n_chunks)),
                dma((n_sub_epochs, n_chunks)),
                dma((2, n_chunks)),
                dma((n_sub_epochs, n_chunks)),
                dma((n_chunks,)),
                dma((n_chunks,)),
            ],
            compiler_params=pltpu.CompilerParams(
                collective_id=0, has_side_effects=True, vmem_limit_bytes=64_000_000),
        )(ratings, mask, user_init.T, item_init.T)
        return users_t.T, items_t.T

    return jax.shard_map(local_run, mesh=mesh, in_specs=(row_spec, row_spec, row_spec, item_spec), out_specs=(row_spec, item_spec), check_vma=False)
```

time: 249 us -> 241 us (0.968)
  Pallas kernels: 244 us -> 237 us
    pallas_call x1, Pallas kernels: 244 us -> 237 us  [local_run(): pl.pallas_call(functools.partial(run, n_blk, eta, lam), out_shape=[jax.Sh...]
where the time goes in v3:
time: 241 us
  Pallas kernels  237 us (98%)
  local copies, waits for them, and re-layouts  3.53 us (1%)
    pallas_call x1, Pallas kernels, local_run(): pl.pallas_call(functools.partial(run, n_blk, eta, lam), out_shape=[jax.Sh...  237 us

profile of v3, /device:TPU:0, one launch (start us, length us, event | category | flops | bytes accessed | tf_op | source)
XLA Modules:
  0.0 241.1 jit_solution(4995693342053800479)
XLA Ops:
  0.6 236.9 %shard_map.59 = (f32[96,1024]{1,0:T(8,128)}, f32[96,1024]{1,0:T(8,128)}) custom-call(f32[1024,4096]{1,0:T(8,128)} %r_hbm.1, s32[1024,4096]{1,0:T(8,128)} %m_hbm.1, f32[96,1024]{1,0:T(8,128)} %bitcast.4, f32[96,1024]{1,0:T(8,128)} %bitcast.5), custom_call_target="tpu_custom_call" | custom-call | tf_op jit(solution)/shard_map/pallas_call | solution.py:297
  237.6 1.8 copy.8
  239.3 1.8 copy.9

commit v4 on v3

--- a/solution.py
+++ b/solution.py
@@ -297,7 +297,7 @@
         users_t, items_t = pl.pallas_call(
             functools.partial(run, n_blk, eta, lam),
             out_shape=[jax.ShapeDtypeStruct((rank, n_users), f32), jax.ShapeDtypeStruct((rank, n_items), f32)],
-            in_specs=[any_space] * 4,
+            in_specs=[pl.BlockSpec(memory_space=pltpu.HBM)] * 4,
             out_specs=[any_space] * 2,
             scratch_shapes=[
                 pltpu.VMEM((n_blk, 2, n_users, half), f32),
@@ -331,7 +331,7 @@
                 dma((n_chunks,)),
             ],
             compiler_params=pltpu.CompilerParams(
-                collective_id=0, has_side_effects=True, vmem_limit_bytes=64_000_000),
+                collective_id=0, has_side_effects=True, vmem_limit_bytes=52_000_000),
         )(ratings, mask, user_init.T, item_init.T)
         return users_t.T, items_t.T
 

time: 241 us -> 243 us (level)
  no operation moved by 1% of the time
where the time goes in v4:
time: 243 us
  Pallas kernels  239 us (98%)
  local copies, waits for them, and re-layouts  3.48 us (1%)
    pallas_call x1, Pallas kernels, local_run(): pl.pallas_call(functools.partial(run, n_blk, eta, lam), out_shape=[jax.Sh...  239 us

profile of v4, /device:TPU:0, one launch (start us, length us, event | category | flops | bytes accessed | tf_op | source)
XLA Modules:
  0.0 242.9 jit_solution(17455328455616657717)
XLA Ops:
  0.6 0.0 copy-start
  0.6 1.0 copy-done
  1.6 0.0 copy-start.1
  1.6 1.0 copy-done.1
  2.6 238.8 %shard_map.59 = (f32[96,1024]{1,0:T(8,128)S(1)}, f32[96,1024]{1,0:T(8,128)S(1)}) custom-call(f32[1024,4096]{1,0:T(8,128)} %r_hbm.1, s32[1024,4096]{1,0:T(8,128)} %m_hbm.1, f32[96,1024]{1,0:T(8,128)S(1)} %bitcast.4, f32[96,1024]{1,0:T(8,128)S(1)} %bitcast.5), custom_call_target="tpu_custom_call" | custom-call | tf_op jit(solution)/shard_map/pallas_call | solution.py:297
  241.5 0.7 copy.8
  242.2 0.7 copy.9
Async XLA Ops:
  0.6 1.0 copy-start
  1.6 1.0 copy-start.1

commit v5 on v4

--- a/solution.py
+++ b/solution.py
@@ -16,8 +16,8 @@
 ROWS = 256
 PIECES = 2
 ORDERS = (
-    ('A0', 'A1', 'A2', 'A3', 'B', 'C0', 'M', 'C1', 'C2', 'C3'),
-    ('A0', 'A1', 'D2', 'D3', 'B', 'C0', 'A2', 'C1', 'A3', 'M'),
+    ('A0', 'B1', 'A1', 'B0', 'A2', 'A3', 'C0', 'M', 'C1', 'C2', 'C3'),
+    ('A0', 'A1', 'D2', 'D3', 'B0', 'C0', 'B1', 'A2', 'C1', 'A3', 'M'),
 )
 MESH = pl.DeviceIdType.MESH
 NT = (((1,), (1,)), ((), ()))
@@ -152,27 +152,27 @@
         for p in range(PIECES):
             part_copy(k, slot, c, p).start()
 
-    def own_part(t, q):
+    def own_part(t, q, part_idx, first):
         if q == 0:
-            @pl.when(t + 1 < n_blk)
-            def _():
-                start_load(t + 1)
-
-            @pl.when(t < n_blk)
-            def _():
-                for copy in load(t, 1):
-                    copy.wait()
-            for c in range(n_chunks):
+            if first:
+                @pl.when(t + 1 < n_blk)
+                def _():
+                    start_load(t + 1)
+
+                @pl.when(t < n_blk)
+                def _():
+                    for copy in load(t, 1):
+                        copy.wait()
+            for c in range(part_idx * n_chunks // 2, (part_idx + 1) * n_chunks // 2):
                 @pl.when(t > 0)
                 def _():
                     edge_own(t - 1, c).wait_recv()
                 v = in_v[t, c]
                 own[:, pl.ds(c * CHUNK, CHUNK)] = v
                 own_bf[0, :, pl.ds(c * CHUNK, CHUNK)] = v.astype(jnp.bfloat16)
-        for c in range(0, half, 256):
-            cols = pl.ds(c, 256)
-            errors(lax.rem(t, n_blk), 1, cols, own_bf[q % 2, :, cols])
-            part[:, cols] = jnp.dot(users_t[...], err[1, :, cols], preferred_element_type=jnp.float32)
+        cols = pl.ds(part_idx * half // 2, half // 2)
+        errors(lax.rem(t, n_blk), 1, cols, own_bf[q % 2, :, cols])
+        part[:, cols] = jnp.dot(users_t[...], err[1, :, cols], preferred_element_type=jnp.float32)
 
     def step_users(t, q):
         k = STEPS * t + q
@@ -241,7 +241,7 @@
                         elif op[0] == 'D' and q > 0:
                             step_items(t, q - 1, c)
                         elif op[0] == 'B':
-                            own_part(t, q)
+                            own_part(t, q, c, op == next(x for x in order if x[0] == 'B'))
                         elif op[0] == 'C':
                             step_items(t, q, c)
                         elif op[0] == 'M':
@@ -294,10 +294,11 @@
         dma = pltpu.SemaphoreType.DMA
         chunk = (rank, CHUNK)
         any_space = pl.BlockSpec(memory_space=pl.ANY)
+        in_hbm = functools.partial(pltpu.with_memory_space_constraint, memory_space=pltpu.HBM)
         users_t, items_t = pl.pallas_call(
             functools.partial(run, n_blk, eta, lam),
             out_shape=[jax.ShapeDtypeStruct((rank, n_users), f32), jax.ShapeDtypeStruct((rank, n_items), f32)],
-            in_specs=[pl.BlockSpec(memory_space=pltpu.HBM)] * 4,
+            in_specs=[any_space] * 4,
             out_specs=[any_space] * 2,
             scratch_shapes=[
                 pltpu.VMEM((n_blk, 2, n_users, half), f32),
@@ -332,7 +333,7 @@
             ],
             compiler_params=pltpu.CompilerParams(
                 collective_id=0, has_side_effects=True, vmem_limit_bytes=52_000_000),
-        )(ratings, mask, user_init.T, item_init.T)
+        )(ratings, mask, in_hbm(user_init.T), in_hbm(item_init.T))
         return users_t.T, items_t.T
 
     return jax.shard_map(local_run, mesh=mesh, in_specs=(row_spec, row_spec, row_spec, item_spec), out_specs=(row_spec, item_spec), check_vma=False)

time: 243 us -> 257 us (1.058)
  Pallas kernels: 239 us -> 252 us
    pallas_call x1, Pallas kernels: 239 us -> 252 us  [local_run(): pl.pallas_call(functools.partial(run, n_blk, eta, lam), out_shape=[jax.Sh...]
where the time goes in v5:
time: 257 us; the launch traced here: 255 us
  Pallas kernels  252 us (98%)
    pallas_call x1, Pallas kernels, local_run(): pl.pallas_call(functools.partial(run, n_blk, eta, lam), out_shape=[jax.Sh...  252 us

profile of v5, /device:TPU:0, one launch (start us, length us, event | category | flops | bytes accessed | tf_op | source)
XLA Modules:
  0.0 254.6 jit_solution(312237986747908240)
XLA Ops:
  0.6 252.4 %shard_map.59 = (f32[96,1024]{1,0:T(8,128)S(1)}, f32[96,1024]{1,0:T(8,128)S(1)}) custom-call(f32[1024,4096]{1,0:T(8,128)} %r_hbm.1, s32[1024,4096]{1,0:T(8,128)} %m_hbm.1, f32[96,1024]{1,0:T(8,128)} %bitcast.6, f32[96,1024]{1,0:T(8,128)} %bitcast.7), custom_call_target="tpu_custom_call" | custom-call | tf_op jit(solution)/shard_map/pallas_call | solution.py:298
  253.1 0.7 copy.8
  253.8 0.7 copy.9

commit v6 on v4

--- a/solution.py
+++ b/solution.py
@@ -294,10 +294,11 @@
         dma = pltpu.SemaphoreType.DMA
         chunk = (rank, CHUNK)
         any_space = pl.BlockSpec(memory_space=pl.ANY)
+        in_hbm = functools.partial(pltpu.with_memory_space_constraint, memory_space=pltpu.HBM)
         users_t, items_t = pl.pallas_call(
             functools.partial(run, n_blk, eta, lam),
             out_shape=[jax.ShapeDtypeStruct((rank, n_users), f32), jax.ShapeDtypeStruct((rank, n_items), f32)],
-            in_specs=[pl.BlockSpec(memory_space=pltpu.HBM)] * 4,
+            in_specs=[any_space] * 4,
             out_specs=[any_space] * 2,
             scratch_shapes=[
                 pltpu.VMEM((n_blk, 2, n_users, half), f32),
@@ -332,7 +333,7 @@
             ],
             compiler_params=pltpu.CompilerParams(
                 collective_id=0, has_side_effects=True, vmem_limit_bytes=52_000_000),
-        )(ratings, mask, user_init.T, item_init.T)
+        )(ratings, mask, in_hbm(user_init.T), in_hbm(item_init.T))
         return users_t.T, items_t.T
 
     return jax.shard_map(local_run, mesh=mesh, in_specs=(row_spec, row_spec, row_spec, item_spec), out_specs=(row_spec, item_spec), check_vma=False)

time: 243 us -> 238 us (0.979)
  Pallas kernels: 239 us -> 236 us
    pallas_call x1, Pallas kernels: 239 us -> 236 us  [local_run(): pl.pallas_call(functools.partial(run, n_blk, eta, lam), out_shape=[jax.Sh...]
where the time goes in v6:
time: 238 us
  Pallas kernels  236 us (99%)
    pallas_call x1, Pallas kernels, local_run(): pl.pallas_call(functools.partial(run, n_blk, eta, lam), out_shape=[jax.Sh...  236 us

profile of v6, /device:TPU:0, one launch (start us, length us, event | category | flops | bytes accessed | tf_op | source)
XLA Modules:
  0.0 237.8 jit_solution(5389116753650727649)
XLA Ops:
  0.6 235.6 %shard_map.59 = (f32[96,1024]{1,0:T(8,128)S(1)}, f32[96,1024]{1,0:T(8,128)S(1)}) custom-call(f32[1024,4096]{1,0:T(8,128)} %r_hbm.1, s32[1024,4096]{1,0:T(8,128)} %m_hbm.1, f32[96,1024]{1,0:T(8,128)} %bitcast.6, f32[96,1024]{1,0:T(8,128)} %bitcast.7), custom_call_target="tpu_custom_call" | custom-call | tf_op jit(solution)/shard_map/pallas_call | solution.py:298
  236.3 0.7 copy.8
  237.0 0.7 copy.9

commit v7 on v6

--- a/solution.py
+++ b/solution.py
@@ -15,9 +15,20 @@
 CHUNK = 128
 ROWS = 256
 PIECES = 2
+MIDDLE = ('A0', 'A1', 'D2', 'D3', 'B', 'C0', 'A2', 'C1', 'A3', 'M')
 ORDERS = (
-    ('A0', 'A1', 'A2', 'A3', 'B', 'C0', 'M', 'C1', 'C2', 'C3'),
-    ('A0', 'A1', 'D2', 'D3', 'B', 'C0', 'A2', 'C1', 'A3', 'M'),
+    (
+        ('A0', 'A1', 'B', 'A2', 'A3', 'C0', 'C1', 'M', 'C2', 'C3'),
+        ('A0', 'B', 'A1', 'A2', 'A3', 'C0', 'M', 'C1', 'C2', 'C3'),
+        ('A0', 'B', 'A1', 'A2', 'A3', 'C0', 'M', 'C1', 'C2', 'C3'),
+        ('A0', 'A1', 'A2', 'A3', 'B', 'C0', 'C1', 'M', 'C2', 'C3'),
+    ),
+    (
+        ('A0', 'A1', 'B', 'C0', 'A2', 'C1', 'A3', 'M'),
+        MIDDLE,
+        MIDDLE,
+        ('A0', 'A1', 'D2', 'D3', 'B', 'C0', 'A2', 'A3', 'C1', 'M', 'C2', 'C3'),
+    ),
 )
 MESH = pl.DeviceIdType.MESH
 NT = (((1,), (1,)), ((), ()))
@@ -230,25 +241,22 @@
         def _():
             for copy in load(t, 0):
                 copy.wait()
-        for core, order in enumerate(ORDERS):
+        for core, orders in enumerate(ORDERS):
             @pl.when(lax.rem(blk, 2) == core)
             def _():
                 for q in range(STEPS):
-                    for op in order:
+                    for op in orders[q]:
                         c = int(op[1:] or 0)
                         if op[0] == 'A':
                             send_part(t, q, c)
-                        elif op[0] == 'D' and q > 0:
-                            step_items(t, q - 1, c)
                         elif op[0] == 'B':
                             own_part(t, q)
                         elif op[0] == 'C':
                             step_items(t, q, c)
-                        elif op[0] == 'M':
+                        elif op[0] == 'D':
+                            step_items(t, q - 1, c)
+                        else:
                             step_users(t, q)
-                for op in order:
-                    if op[0] == 'D':
-                        step_items(t, STEPS - 1, int(op[1:]))
         return carry
 
     lax.fori_loop(0, n_sub_epochs, sub_epoch, 0)

time: 238 us -> 249 us (1.046)
  Pallas kernels: 236 us -> 246 us
    pallas_call x1, Pallas kernels: 236 us -> 246 us  [local_run(): pl.pallas_call(functools.partial(run, n_blk, eta, lam), out_shape=[jax.Sh...]
where the time goes in v7:
time: 249 us; the launch traced here: 248 us
  Pallas kernels  246 us (99%)
    pallas_call x1, Pallas kernels, local_run(): pl.pallas_call(functools.partial(run, n_blk, eta, lam), out_shape=[jax.Sh...  246 us

profile of v7, /device:TPU:0, one launch (start us, length us, event | category | flops | bytes accessed | tf_op | source)
XLA Modules:
  0.0 248.4 jit_solution(2192120196007123139)
XLA Ops:
  0.6 246.2 %shard_map.59 = (f32[96,1024]{1,0:T(8,128)S(1)}, f32[96,1024]{1,0:T(8,128)S(1)}) custom-call(f32[1024,4096]{1,0:T(8,128)} %r_hbm.1, s32[1024,4096]{1,0:T(8,128)} %m_hbm.1, f32[96,1024]{1,0:T(8,128)} %bitcast.6, f32[96,1024]{1,0:T(8,128)} %bitcast.7), custom_call_target="tpu_custom_call" | custom-call | tf_op jit(solution)/shard_map/pallas_call | solution.py:306
  246.9 0.7 copy.8
  247.6 0.7 copy.9

commit v8 on v6

--- a/solution.py
+++ b/solution.py
@@ -26,7 +26,7 @@
 def run(n_blk, eta, lam, r_hbm, m_hbm, u_hbm, v_hbm, u_out, v_out,
         rate, known, err, users, users_bf, users_t, own, own_bf, own_next, part, send_p, recv_p,
         peer_v, in_v, v_start, edge_f, edge_b,
-        load_sem, uv_sem, p_send, p_recv, v_send, v_recv,
+        load_sem, first_sem, uv_sem, p_send, p_recv, v_send, v_recv,
         ef_send, ef_recv, eb_send, eb_recv, el_send, el_recv):
     rank, n_users = users.shape
     half = own.shape[1]
@@ -47,6 +47,13 @@
             for j, (src, dst) in enumerate(((r_hbm, rate), (m_hbm, known)))
         ]
 
+    def first_load(c):
+        col = pl.multiple_of(blk * (2 * half) + other * half + c * CHUNK, CHUNK)
+        return [
+            pltpu.make_async_copy(src.at[:, pl.ds(col, CHUNK)], dst.at[0, 0, :, pl.ds(c * CHUNK, CHUNK)], first_sem.at[c, j])
+            for j, (src, dst) in enumerate(((r_hbm, rate), (m_hbm, known)))
+        ]
+
     def start_load(t):
         for role in range(2):
             for copy in load(t, role):
@@ -56,8 +63,9 @@
     v_copy = pltpu.make_async_copy(v_hbm, v_start, uv_sem.at[1])
     u_copy.start()
     v_copy.start()
-    for copy in load(0, 0):
-        copy.start()
+    for c in range(n_chunks):
+        for copy in first_load(c):
+            copy.start()
 
     barrier = pltpu.get_barrier_semaphore()
     friends = [(blk, other), (down, me), (down, other), (up, me), (up, other)]
@@ -81,10 +89,6 @@
         theirs = pl.ds(pl.multiple_of(other * half + c * CHUNK, CHUNK), CHUNK)
         in_v[0, c] = v_start[:, mine(c)]
         peer_v[0, c] = v_start[:, theirs].astype(jnp.bfloat16)
-    for copy in load(0, 0):
-        copy.wait()
-    for copy in load(0, 1):
-        copy.start()
     pl.semaphore_wait(barrier, len(friends))
 
     def remote(src, dst, send, recv, s, b):
@@ -106,9 +110,9 @@
         slot = lax.rem(t, 2)
         return remote(edge_f.at[slot, c], in_v.at[t + 1, c], ef_send.at[slot, c], ef_recv.at[t, c], me, down)
 
-    def edge_peer(t, c):
-        slot = lax.rem(t, 2)
-        return remote(edge_b.at[slot, c], peer_v.at[STEPS * (t + 1), c], eb_send.at[slot, c], eb_recv.at[t, c], other, down)
+    def edge_peer(t, c, p):
+        slot, at = lax.rem(t, 2), pl.ds(p * piece, piece)
+        return remote(edge_b.at[slot, c, at], peer_v.at[STEPS * (t + 1), c, at], eb_send.at[slot, c, p], eb_recv.at[t, c, p], other, down)
 
     def edge_last(t, c):
         slot = lax.rem(t, 2)
@@ -132,9 +136,18 @@
     def send_part(t, q, c):
         k, slot = STEPS * t + q, q % 2
         if q == 0:
+            @pl.when(t == 0)
+            def _():
+                for copy in first_load(c):
+                    copy.wait()
+                if c == 1:
+                    for copy in load(0, 1):
+                        copy.start()
+
             @pl.when(t > 0)
             def _():
-                edge_peer(t - 1, c).wait_recv()
+                for p in range(PIECES):
+                    edge_peer(t - 1, c, p).wait_recv()
         else:
             for p in range(PIECES):
                 item_copy(k - 1, q - 1, c, p).wait_recv()
@@ -199,7 +212,8 @@
             @pl.when(t > 1)
             def _():
                 edge_own(t - 2, c).wait_send()
-                edge_peer(t - 2, c).wait_send()
+                for p in range(PIECES):
+                    edge_peer(t - 2, c, p).wait_send()
         for p in range(PIECES):
             at = pl.ds(p * piece, piece)
             part_copy(k, slot, c, p).wait_recv()
@@ -212,12 +226,15 @@
                 own[at, cols] = v
                 own_bf[(q + 1) % 2, at, cols] = v_bf
             else:
+                edge_b[edge_slot, c, at] = v_bf
+
+                @pl.when(t < n_sub_epochs - 1)
+                def _():
+                    edge_peer(t, c, p).start()
                 edge_f[edge_slot, c, at] = v
-                edge_b[edge_slot, c, at] = v_bf
         if q == STEPS - 1:
             @pl.when(t < n_sub_epochs - 1)
             def _():
-                edge_peer(t, c).start()
                 edge_own(t, c).start()
 
             @pl.when(t == n_sub_epochs - 1)
@@ -267,7 +284,8 @@
             for q in range(STEPS - 1):
                 item_copy(STEPS * end + q, q, c, p).wait_send()
         edge_own(end - 1, c).wait_send()
-        edge_peer(end - 1, c).wait_send()
+        for p in range(PIECES):
+            edge_peer(end - 1, c, p).wait_send()
         edge_end(end, c).wait_send()
         edge_last(end, c).wait_send()
     u_back.wait()
@@ -319,6 +337,7 @@
                 pltpu.VMEM((2, n_chunks) + chunk, f32),
                 pltpu.VMEM((2, n_chunks) + chunk, bf16),
                 dma((n_blk, 2, 2)),
+                dma((n_chunks, 2)),
                 dma((2,)),
                 dma((2, n_chunks, PIECES)),
                 dma((2, n_chunks, PIECES)),
@@ -326,8 +345,8 @@
                 dma((n_chunks, PIECES)),
                 dma((2, n_chunks)),
                 dma((n_sub_epochs, n_chunks)),
-                dma((2, n_chunks)),
-                dma((n_sub_epochs, n_chunks)),
+                dma((2, n_chunks, PIECES)),
+                dma((n_sub_epochs, n_chunks, PIECES)),
                 dma((n_chunks,)),
                 dma((n_chunks,)),
             ],

time: 238 us -> 243 us (1.021)
  Pallas kernels: 236 us -> 241 us
    pallas_call x1, Pallas kernels: 236 us -> 241 us  [local_run(): pl.pallas_call(functools.partial(run, n_blk, eta, lam), out_shape=[jax.Sh...]
where the time goes in v8:
time: 243 us
  Pallas kernels  241 us (99%)
    pallas_call x1, Pallas kernels, local_run(): pl.pallas_call(functools.partial(run, n_blk, eta, lam), out_shape=[jax.Sh...  241 us

profile of v8, /device:TPU:0, one launch (start us, length us, event | category | flops | bytes accessed | tf_op | source)
XLA Modules:
  0.0 243.4 jit_solution(16286376845495015527)
XLA Ops:
  0.6 241.3 %shard_map.59 = (f32[96,1024]{1,0:T(8,128)S(1)}, f32[96,1024]{1,0:T(8,128)S(1)}) custom-call(f32[1024,4096]{1,0:T(8,128)} %r_hbm.1, s32[1024,4096]{1,0:T(8,128)} %m_hbm.1, f32[96,1024]{1,0:T(8,128)} %bitcast.6, f32[96,1024]{1,0:T(8,128)} %bitcast.7), custom_call_target="tpu_custom_call" | custom-call | tf_op jit(solution)/shard_map/pallas_call | solution.py:316
  241.9 0.7 copy.8
  242.7 0.7 copy.9

commit v9 on v8

--- a/solution.py
+++ b/solution.py
@@ -110,9 +110,9 @@
         slot = lax.rem(t, 2)
         return remote(edge_f.at[slot, c], in_v.at[t + 1, c], ef_send.at[slot, c], ef_recv.at[t, c], me, down)
 
-    def edge_peer(t, c, p):
-        slot, at = lax.rem(t, 2), pl.ds(p * piece, piece)
-        return remote(edge_b.at[slot, c, at], peer_v.at[STEPS * (t + 1), c, at], eb_send.at[slot, c, p], eb_recv.at[t, c, p], other, down)
+    def edge_peer(t, c):
+        slot = lax.rem(t, 2)
+        return remote(edge_b.at[slot, c], peer_v.at[STEPS * (t + 1), c], eb_send.at[slot, c], eb_recv.at[t, c], other, down)
 
     def edge_last(t, c):
         slot = lax.rem(t, 2)
@@ -146,8 +146,7 @@
 
             @pl.when(t > 0)
             def _():
-                for p in range(PIECES):
-                    edge_peer(t - 1, c, p).wait_recv()
+                edge_peer(t - 1, c).wait_recv()
         else:
             for p in range(PIECES):
                 item_copy(k - 1, q - 1, c, p).wait_recv()
@@ -212,8 +211,7 @@
             @pl.when(t > 1)
             def _():
                 edge_own(t - 2, c).wait_send()
-                for p in range(PIECES):
-                    edge_peer(t - 2, c, p).wait_send()
+                edge_peer(t - 2, c).wait_send()
         for p in range(PIECES):
             at = pl.ds(p * piece, piece)
             part_copy(k, slot, c, p).wait_recv()
@@ -226,15 +224,12 @@
                 own[at, cols] = v
                 own_bf[(q + 1) % 2, at, cols] = v_bf
             else:
+                edge_f[edge_slot, c, at] = v
                 edge_b[edge_slot, c, at] = v_bf
-
-                @pl.when(t < n_sub_epochs - 1)
-                def _():
-                    edge_peer(t, c, p).start()
-                edge_f[edge_slot, c, at] = v
         if q == STEPS - 1:
             @pl.when(t < n_sub_epochs - 1)
             def _():
+                edge_peer(t, c).start()
                 edge_own(t, c).start()
 
             @pl.when(t == n_sub_epochs - 1)
@@ -284,8 +279,7 @@
             for q in range(STEPS - 1):
                 item_copy(STEPS * end + q, q, c, p).wait_send()
         edge_own(end - 1, c).wait_send()
-        for p in range(PIECES):
-            edge_peer(end - 1, c, p).wait_send()
+        edge_peer(end - 1, c).wait_send()
         edge_end(end, c).wait_send()
         edge_last(end, c).wait_send()
     u_back.wait()
@@ -345,8 +339,8 @@
                 dma((n_chunks, PIECES)),
                 dma((2, n_chunks)),
                 dma((n_sub_epochs, n_chunks)),
-                dma((2, n_chunks, PIECES)),
-                dma((n_sub_epochs, n_chunks, PIECES)),
+                dma((2, n_chunks)),
+                dma((n_sub_epochs, n_chunks)),
                 dma((n_chunks,)),
                 dma((n_chunks,)),
             ],

time: 243 us -> 243 us (level)
  no operation moved by 1% of the time
where the time goes in v9:
time: 243 us
  Pallas kernels  240 us (99%)
    pallas_call x1, Pallas kernels, local_run(): pl.pallas_call(functools.partial(run, n_blk, eta, lam), out_shape=[jax.Sh...  240 us

profile of v9, /device:TPU:0, one launch (start us, length us, event | category | flops | bytes accessed | tf_op | source)
XLA Modules:
  0.0 242.5 jit_solution(7467058491299650599)
XLA Ops:
  0.6 240.4 %shard_map.59 = (f32[96,1024]{1,0:T(8,128)S(1)}, f32[96,1024]{1,0:T(8,128)S(1)}) custom-call(f32[1024,4096]{1,0:T(8,128)} %r_hbm.1, s32[1024,4096]{1,0:T(8,128)} %m_hbm.1, f32[96,1024]{1,0:T(8,128)} %bitcast.6, f32[96,1024]{1,0:T(8,128)} %bitcast.7), custom_call_target="tpu_custom_call" | custom-call | tf_op jit(solution)/shard_map/pallas_call | solution.py:310
  241.0 0.7 copy.8
  241.8 0.7 copy.9

commit v10 on v7

--- a/solution.py
+++ b/solution.py
@@ -15,19 +15,15 @@
 CHUNK = 128
 ROWS = 256
 PIECES = 2
+FIRST = ('A0', 'A1', 'A2', 'A3', 'B', 'C0', 'M', 'C1', 'C2', 'C3')
 MIDDLE = ('A0', 'A1', 'D2', 'D3', 'B', 'C0', 'A2', 'C1', 'A3', 'M')
 ORDERS = (
-    (
-        ('A0', 'A1', 'B', 'A2', 'A3', 'C0', 'C1', 'M', 'C2', 'C3'),
-        ('A0', 'B', 'A1', 'A2', 'A3', 'C0', 'M', 'C1', 'C2', 'C3'),
-        ('A0', 'B', 'A1', 'A2', 'A3', 'C0', 'M', 'C1', 'C2', 'C3'),
-        ('A0', 'A1', 'A2', 'A3', 'B', 'C0', 'C1', 'M', 'C2', 'C3'),
-    ),
+    (FIRST, FIRST, FIRST, FIRST),
     (
         ('A0', 'A1', 'B', 'C0', 'A2', 'C1', 'A3', 'M'),
         MIDDLE,
         MIDDLE,
-        ('A0', 'A1', 'D2', 'D3', 'B', 'C0', 'A2', 'A3', 'C1', 'M', 'C2', 'C3'),
+        ('A0', 'A1', 'D2', 'D3', 'B', 'C0', 'C1', 'A2', 'A3', 'M', 'C2', 'C3'),
     ),
 )
 MESH = pl.DeviceIdType.MESH

time: 249 us -> 241 us (0.968)
  Pallas kernels: 246 us -> 239 us
    pallas_call x1, Pallas kernels: 246 us -> 239 us  [local_run(): pl.pallas_call(functools.partial(run, n_blk, eta, lam), out_shape=[jax.Sh...]
where the time goes in v10:
time: 241 us
  Pallas kernels  239 us (99%)
    pallas_call x1, Pallas kernels, local_run(): pl.pallas_call(functools.partial(run, n_blk, eta, lam), out_shape=[jax.Sh...  239 us

profile of v10, /device:TPU:0, one launch (start us, length us, event | category | flops | bytes accessed | tf_op | source)
XLA Modules:
  0.0 240.7 jit_solution(7756110248472519810)
XLA Ops:
  0.6 238.5 %shard_map.59 = (f32[96,1024]{1,0:T(8,128)S(1)}, f32[96,1024]{1,0:T(8,128)S(1)}) custom-call(f32[1024,4096]{1,0:T(8,128)} %r_hbm.1, s32[1024,4096]{1,0:T(8,128)} %m_hbm.1, f32[96,1024]{1,0:T(8,128)} %bitcast.6, f32[96,1024]{1,0:T(8,128)} %bitcast.7), custom_call_target="tpu_custom_call" | custom-call | tf_op jit(solution)/shard_map/pallas_call | solution.py:302
  239.2 0.7 copy.8
  239.9 0.7 copy.9
